TPU v7x, 32 devices: a whole 2x2x4 slice. The times are simulated.
32 devices in a mesh: freq: 4 (over y, x), band: 8 (over z, core).
Axes of the slice: x: 2, y: 2, z: 4, core: 2. Of those that a mesh axis runs over, the one named last changes fastest.
Arguments:
- pair_density: bfloat16 [1024, 2, 8192], P(('freq', 'band')), may hold values from -6 to 6
- trial_vectors: bfloat16 [16, 2, 64, 8192], P('freq', None, None, 'band'), may hold values from -6 to 6
- frequency: float32 [16], P('freq'), may hold values from 0.05 to 20
- val_energy: float32 [32], replicated, may hold values from -3 to -0.1
- cond_energy: float32 [32], replicated, may hold values from 0.1 to 4
- pair_index: int32 [1024], P(('freq', 'band')), may hold values from 0 to 1023, each once
Outputs:
- images: float32 [16, 2, 64, 8192], P('freq', None, None, 'band')
- subspace: float32 [16, 2, 64, 64], P('freq')
Inputs may be any that keep to these rules, and one draw needn't show every extreme that they name: `pair_index`: every pair number 0 to 1023 appears exactly once.
All inputs are finite; a program needn't handle non-finite values.
Results may differ from a plain program's by a relative error of at most 0.0085.
Values may be sent and summed in bfloat16 or wider, within the bound.
A program may use at most 128 MiB of HBM per device.

v0:
```python
import functools
import math

import jax
import jax.numpy as jnp
from jax import lax
from jax.experimental import pallas as pl
from jax.experimental.pallas import tpu as pltpu
from jax.sharding import PartitionSpec as P

MESH = pl.DeviceIdType.MESH
F32 = jnp.float32
BF16 = jnp.bfloat16


def kernel(
    groups, members, chunks, freqs, vecs, rows, grid_here, prefactor, inv_grid,
    dens, trial, frequency, val_energy, cond_energy, pair_index,
    images, sub,
    held, mix, delta_own, freq_row, deltas, cols, part_out, part_in, own, ring_out, ring_in, scaled, acc,
    sem_as, sem_ar, sem_fs, sem_fr, sem_ds, sem_dr, sem_es, sem_er,
    sem_ps, sem_pr, sem_rs, sem_rr, sem_gs, sem_gr, sem_hs, sem_hr,
):
    f = lax.axis_index("freq")
    b = lax.axis_index("band")
    chips = members // 2
    piece = rows // chunks
    zc = b // 2
    core = b % 2
    width = freqs * 2 * vecs
    chunk_rows = groups * members * piece
    slot = groups * piece
    partner = zc * 2 + (1 - core)

    def remote(src, dst, send, recv, freq_id, band_id):
        return pltpu.make_async_remote_copy(
            src_ref=src, dst_ref=dst, send_sem=send, recv_sem=recv,
            device_id=(freq_id, band_id), device_id_type=MESH,
        )

    barrier = pltpu.get_barrier_semaphore()
    for s in range(1, members):
        pl.semaphore_signal(barrier, inc=1, device_id=(f, (b + s) % members), device_id_type=MESH)
    for s in range(1, groups):
        pl.semaphore_signal(barrier, inc=1, device_id=((f + s) % groups, b), device_id_type=MESH)
    pl.semaphore_wait(barrier, members + groups - 2)

    def waves(c, to):
        return dens.at[c, :, :, pl.ds(pl.multiple_of(to * grid_here, 128), grid_here)]

    sends = []

    def go(copy):
        copy.start()
        sends.append(copy)

    for c in range(chunks):
        pltpu.make_async_copy(waves(c, b), held.at[c, f, b], sem_ar.at[c, b]).start()
        go(remote(waves(c, partner), held.at[c, f, b], sem_as.at[c, 0], sem_ar.at[c, b], f, partner))
    def exchange(c):
        for r in range(1, chips):
            for k in range(2):
                to = (zc + r) % chips * 2 + (core + k) % 2
                go(remote(waves(c, to), held.at[c, f, b], sem_as.at[c, 2 * r + k], sem_ar.at[c, b], f, to))

    cond_count = cond_energy.shape[0]
    val_count = val_energy.shape[0]
    index = pair_index[...]
    rest_index = index
    val_pick = jnp.full(index.shape, val_energy[0], F32)
    for v in range(1, val_count):
        above = index >= v * cond_count
        val_pick = jnp.where(above, val_energy[v], val_pick)
        rest_index = jnp.where(above, index - v * cond_count, rest_index)
    cond_pick = jnp.full(index.shape, cond_energy[0], F32)
    for v in range(1, cond_count):
        cond_pick = jnp.where(rest_index == v, cond_energy[v], cond_pick)
    delta_own[...] = jnp.ones_like(delta_own)
    delta_own[0:1, 0:rows] = cond_pick - val_pick
    for q in range(freqs):
        freq_row[:, q * 2 * vecs : (q + 1) * 2 * vecs] = jnp.full((1, 2 * vecs), frequency[q], F32)
    pltpu.make_async_copy(delta_own, deltas.at[f, b], sem_dr.at[b]).start()
    for s in range(1, members):
        to = (b + s) % members
        go(remote(delta_own, deltas.at[f, b], sem_ds.at[s], sem_dr.at[b], f, to))

    for q in range(freqs):
        lo, hi = q * 2 * vecs, (q * 2 + 1) * vecs
        top = trial[lo : lo + vecs, :]
        low = trial[hi : hi + vecs, :]
        mix[lo : lo + vecs, 0:grid_here] = top
        mix[lo : lo + vecs, grid_here:] = low
        mix[hi : hi + vecs, 0:grid_here] = low
        mix[hi : hi + vecs, grid_here:] = -top

    square_groups = groups == 4
    xx, yy = f % 2, f // 2
    fx, fy = yy * 2 + (1 - xx), (1 - yy) * 2 + xx
    fd = (1 - yy) * 2 + (1 - xx)

    def piece_copy(c, g, z, lane, peer):
        ref = held.at[c, g, pl.ds(2 * z, 2)]
        return remote(ref, ref, sem_fs.at[c, lane, z], sem_fr.at[c, lane, z], peer, b)

    def whole(c, g, lane, peer):
        return remote(held.at[c, g], held.at[c, g], sem_fs.at[c, lane, 0], sem_fr.at[c, lane, 0], peer, b)

    def spread(c, offsets):
        for r in offsets:
            z = (zc + r) % chips
            for k in range(2):
                j = z * 2 + k
                pltpu.make_async_copy(waves(c, 0), held.at[c, f, j], sem_ar.at[c, j]).wait()
            if square_groups:
                go(piece_copy(c, f, z, 0, fx))
                go(piece_copy(c, f, z, 1, fy))
        if not square_groups and offsets[-1] == chips - 1:
            for s in range(1, groups):
                go(whole(c, f, s, (f + s) % groups))

    def relay(c):
        if square_groups:
            for r in range(chips):
                z = (zc + r) % chips
                if r % 2 == 0:
                    piece_copy(c, fx, z, 0, fx).wait_recv()
                    go(piece_copy(c, fx, z, 2, fy))
                else:
                    piece_copy(c, fy, z, 1, fy).wait_recv()
                    go(piece_copy(c, fy, z, 3, fx))

    def arrive(c):
        if square_groups:
            for r in range(chips):
                z = (zc + r) % chips
                if r % 2 == 0:
                    piece_copy(c, fy, z, 1, fy).wait_recv()
                    piece_copy(c, fd, z, 2, fy).wait_recv()
                else:
                    piece_copy(c, fx, z, 0, fx).wait_recv()
                    piece_copy(c, fd, z, 3, fx).wait_recv()
        else:
            for s in range(1, groups):
                src = (f + groups - s) % groups
                whole(c, src, s, src).wait_recv()

    def pass_deltas():
        for j in range(members):
            pltpu.make_async_copy(delta_own, deltas.at[f, j], sem_dr.at[j]).wait()
        for s in range(1, groups):
            go(remote(deltas.at[f], deltas.at[f], sem_es.at[s], sem_er.at[s], (f + s) % groups, b))

    def columns():
        for s in range(1, groups):
            src = (f + groups - s) % groups
            remote(deltas.at[src], deltas.at[src], sem_es.at[s], sem_er.at[s], src, b).wait_recv()
        for g in range(groups):
            for j in range(members):
                turned = jnp.transpose(deltas[g, j])
                at = (g * members + j) * piece
                for c in range(chunks):
                    cols[c, at : at + piece, :] = turned[c * piece : (c + 1) * piece, :]

    def weights(column):
        ratio = column / (column * column + freq_row[...] * freq_row[...])
        return (-4.0 * prefactor * ratio).astype(BF16).astype(F32)

    def cross(j):
        arrive(j)
        over_grid = (((1,), (1,)), ((), ()))
        real = held[j, :, :, 0].reshape(chunk_rows, grid_here)
        imag = held[j, :, :, 1].reshape(chunk_rows, grid_here)
        own[...] = (
            lax.dot_general(real, mix[:, 0:grid_here], over_grid, preferred_element_type=F32)
            + lax.dot_general(imag, mix[:, grid_here:], over_grid, preferred_element_type=F32)
        ).reshape(2, chips, chunk_rows // members, width)
        part_out[j] = own[1 - core].astype(BF16)
        go(remote(part_out.at[j], part_in.at[j], sem_ps.at[j], sem_pr.at[j], f, partner))
        remote(part_out.at[j], part_in.at[j], sem_ps.at[j], sem_pr.at[j], f, partner).wait_recv()
        total = own[core] + part_in[j].astype(F32)
        ring_out[j] = total.astype(BF16)
        for s in range(1, chips):
            to = (zc + s) % chips
            go(remote(ring_out.at[j, to], ring_in.at[j, s], sem_rs.at[j, s], sem_rr.at[j, s], f, to * 2 + core))

    def scale(j):
        total = ring_out[j, zc].astype(F32)
        for s in range(1, chips):
            src = (zc + chips - s) % chips
            remote(ring_out.at[j, zc], ring_in.at[j, s], sem_rs.at[j, s], sem_rr.at[j, s], f, src * 2 + core).wait_recv()
            total = total + ring_in[j, s].astype(F32)
        q = core * chips + zc
        column = cols[j, pl.ds(pl.multiple_of(q * slot, 8), slot), 0:1]
        scaled[j, core, zc] = (weights(column) * total).astype(BF16)
        for s in range(1, chips):
            to = (zc + s) % chips
            go(remote(scaled.at[j, core, zc], scaled.at[j, core, zc], sem_gs.at[j, s], sem_gr.at[j, s], f, to * 2 + core))

    def share(j):
        for s in range(1, chips):
            src = (zc + chips - s) % chips
            remote(scaled.at[j, core, src], scaled.at[j, core, src], sem_gs.at[j, s], sem_gr.at[j, s], f, src * 2 + core).wait_recv()
        go(remote(scaled.at[j, core], scaled.at[j, core], sem_hs.at[j], sem_hr.at[j], f, partner))

    def image(j):
        remote(scaled.at[j, 1 - core], scaled.at[j, 1 - core], sem_hs.at[j], sem_hr.at[j], f, partner).wait_recv()
        flat = scaled[j].reshape(chunk_rows, width)
        flat32 = flat.astype(F32)
        lane = lax.broadcasted_iota(jnp.int32, (1, 2 * vecs), 1)
        sign = jnp.where(lane < vecs, -1.0, 1.0)
        turned = jnp.concatenate(
            [
                pltpu.roll(flat32[:, q * 2 * vecs : (q + 1) * 2 * vecs], vecs, 1) * sign
                for q in range(freqs)
            ],
            axis=1,
        ).astype(BF16)
        over_rows = (((0,), (0,)), ((), ()))
        real = held[j, :, :, 0].reshape(chunk_rows, grid_here)
        imag = held[j, :, :, 1].reshape(chunk_rows, grid_here)
        term = lax.dot_general(flat, real, over_rows, preferred_element_type=F32) + lax.dot_general(
            turned, imag, over_rows, preferred_element_type=F32
        )
        column = cols[j, :, 0:1]
        crossing = (flat32 / weights(column)).astype(BF16)
        for q in range(freqs):
            lo, hi = q * 2 * vecs, (q + 1) * 2 * vecs
            square = lax.dot_general(
                crossing[:, lo:hi], flat[:, lo:hi], over_rows, preferred_element_type=F32
            )
            if j == 0:
                acc[q] = square
            else:
                acc[q] = acc[q] + square
        if j == 0:
            images[...] = term
        else:
            images[...] = images[...] + term

    exchange(0)
    for c in range(chunks):
        spread(c, (0,))
    pass_deltas()
    for t in range(chunks + 4):
        if t + 1 < chunks:
            exchange(t + 1)
        if t < chunks:
            spread(t, range(1, chips))
        if t == 0:
            columns()
        if 0 <= t - 1 < chunks:
            relay(t - 1)
        if 0 <= t - 3 < chunks:
            scale(t - 3)
        if 0 <= t - 2 < chunks:
            cross(t - 2)
        if 0 <= t - 4 < chunks:
            share(t - 4)
            image(t - 4)

    for q in range(freqs):
        square = acc[q]
        lo, hi = q * 2 * vecs, (q * 2 + 1) * vecs
        sub[lo : lo + vecs, :] = (square[0:vecs, 0:vecs] + square[vecs:, vecs:]) * inv_grid
        sub[hi : hi + vecs, :] = (square[0:vecs, vecs:] - square[vecs:, 0:vecs]) * inv_grid

    for copy in sends:
        copy.wait_send()


def shards(pair_density, trial_vectors, frequency, val_energy, cond_energy, pair_index):
    groups = lax.axis_size("freq")
    members = lax.axis_size("band")
    rows = pair_density.shape[0]
    freqs, _, vecs, grid_here = trial_vectors.shape
    pair_count = rows * groups * members
    grid_count = grid_here * members
    prefactor = 1.0 / math.sqrt(2.0 * grid_count * pair_count)
    width = freqs * 2 * vecs
    chips = members // 2
    chunks = rows // 8
    piece = rows // chunks
    slot = groups * piece
    dens = jnp.transpose(
        pair_density.reshape(chunks, piece, 2, grid_count), (0, 2, 1, 3)
    )
    trial = trial_vectors.reshape(width, grid_here)
    dma = pltpu.SemaphoreType.DMA
    vmem = pl.BlockSpec(memory_space=pltpu.VMEM)
    smem = pl.BlockSpec(memory_space=pltpu.SMEM)
    images, sub = pl.pallas_call(
        functools.partial(
            kernel, groups, members, chunks, freqs, vecs, rows, grid_here, prefactor, 1.0 / grid_count
        ),
        out_shape=(
            jax.ShapeDtypeStruct((width, grid_here), F32),
            jax.ShapeDtypeStruct((width, vecs), F32),
        ),
        in_specs=[vmem] * 2 + [smem] * 3 + [vmem],
        out_specs=(vmem, vmem),
        scratch_shapes=[
            pltpu.VMEM((chunks, groups, members, 2, piece, grid_here), BF16),
            pltpu.VMEM((width, 2 * grid_here), BF16),
            pltpu.VMEM((8, 128), F32),
            pltpu.VMEM((1, width), F32),
            pltpu.VMEM((groups, members, 8, 128), F32),
            pltpu.VMEM((chunks, members * slot, 8), F32),
            pltpu.VMEM((chunks, chips, slot, width), BF16),
            pltpu.VMEM((chunks, chips, slot, width), BF16),
            pltpu.VMEM((2, chips, slot, width), F32),
            pltpu.VMEM((chunks, chips, slot, width), BF16),
            pltpu.VMEM((chunks, chips, slot, width), BF16),
            pltpu.VMEM((chunks, 2, chips, slot, width), BF16),
            pltpu.VMEM((freqs, 2 * vecs, 2 * vecs), F32),
            dma((chunks, members)), dma((chunks, members)),
            dma((chunks, groups, chips)), dma((chunks, groups, chips)),
            dma((members,)), dma((members,)),
            dma((groups,)), dma((groups,)),
            dma((chunks,)), dma((chunks,)),
            dma((chunks, chips)), dma((chunks, chips)),
            dma((chunks, chips)), dma((chunks, chips)),
            dma((chunks,)), dma((chunks,)),
        ],
        compiler_params=pltpu.CompilerParams(
            collective_id=0, has_side_effects=True, vmem_limit_bytes=56 * 1024 * 1024
        ),
    )(dens, trial, frequency, val_energy, cond_energy, pair_index[None, :])
    return (
        images.reshape(freqs, 2, vecs, grid_here),
        sub.reshape(freqs, 2, vecs, vecs),
    )


def solution(mesh):
    return jax.shard_map(
        shards,
        mesh=mesh,
        in_specs=(
            P(("freq", "band"), None, None),
            P("freq", None, None, "band"),
            P("freq"),
            P(),
            P(),
            P(("freq", "band")),
        ),
        out_specs=(P("freq", None, None, "band"), P("freq", None, None, None)),
        check_vma=False,
    )
```

profile of v0, /device:TPU:3, one launch (start us, length us, event | category | flops | bytes accessed | tf_op | source)
XLA Modules:
  0.0 78.3 jit_solution(7312525875353971030)
XLA Ops:
  0.6 2.8 %copy.13 = bf16[4,8,2,8192]{3,1,2,0:T(8,128)(2,1)} copy(bf16[4,8,2,8192]{3,2,1,0:T(2,128)(2,1)} %bitcast.11) | data formatting | bytes 2097152 | tf_op jit(solution)/shard_map/reshape | solution.py:285
  3.4 71.0 %shard_map.77 = (f32[512,1024]{1,0:T(8,128)}, f32[512,64]{1,0:T(8,128)}) custom-call(bf16[4,2,8,8192]{3,2,1,0:T(8,128)(2,1)} %bitcast.8, bf16[512,1024]{1,0:T(8,128)(2,1)} %bitcast.10, f32[4]{0:T(128)} %frequency.1, f32[32]{0:T(128)} %val_energy.1, f32[32]{0:T(128)} %cond_energy.1, s32[1,32]{1,0:T(1,128)} %bitcast.13), custom_call_target="tpu_custom_call" | custom-call | tf_op jit(solution)/shard_map/pallas_call | solution.py:291
  74.4 0.0 copy-start
  74.4 3.2 %copy.16 = f32[4,2,64,1024]{3,2,1,0:T(8,128)} copy(f32[4,2,64,1024]{3,2,1,0:T(8,128)} %bitcast.9) | data formatting | bytes 4194304
  77.6 0.0 copy-done
  77.6 0.7 copy.17
Async XLA Ops:
  74.4 3.2 %copy-start = (f32[512,64]{1,0:T(8,128)S(1)}, f32[512,64]{1,0:T(8,128)}, u32[]{:S(2)}) copy-start(f32[512,64]{1,0:T(8,128)} %get-tuple-element.5) | copy-start | bytes 393220
where the time goes:
time: 78.6 us; the launch traced here: 78.3 us
  Pallas kernels  71 us (90%)
  local copies, waits for them, and re-layouts  6.68 us (8%)
    pallas_call x1, Pallas kernels, shards(): pl.pallas_call(functools.partial(kernel, groups, members, chunks, freqs,...  71 us
    unnamed x4, local copies, waits for them, and re-layouts  3.91 us
    reshape x1, local copies, waits for them, and re-layouts, shards(): pair_density.reshape(chunks, piece, 2, grid_count)  2.78 us

commit v1 on v0

v1 whole, which is shorter than its diff:
```python
import functools
import math

import jax
import jax.numpy as jnp
from jax import lax
from jax.experimental import pallas as pl
from jax.experimental.pallas import tpu as pltpu
from jax.sharding import PartitionSpec as P

MESH = pl.DeviceIdType.MESH
F32 = jnp.float32
BF16 = jnp.bfloat16


def kernel(
    groups, members, chunks, freqs, vecs, rows, grid_here, prefactor, inv_grid,
    dens, trial, frequency, val_energy, cond_energy, pair_index,
    images, sub,
    raw, packed, total_own, held, both, delta_own, freq_row, deltas, cols, ring_out, ring_in, scaled, acc,
    other, late_out, late_in, sub_out, sub_in,
    sem_in, sem_out, sem_as, sem_ar, sem_os, sem_or, sem_fs, sem_fr, sem_ds, sem_dr, sem_es, sem_er,
    sem_rs, sem_rr, sem_gs, sem_gr, sem_is, sem_ir,
):
    f = lax.axis_index("freq")
    b = lax.axis_index("band")
    chips = members // 2
    piece = rows // chunks
    zc = b // 2
    core = b % 2
    width = freqs * 2 * vecs
    slot = groups * piece
    chunk_rows = chips * slot
    wide = 2 * grid_here
    partner = zc * 2 + (1 - core)

    def remote(src, dst, send, recv, freq_id, band_id):
        return pltpu.make_async_remote_copy(
            src_ref=src, dst_ref=dst, send_sem=send, recv_sem=recv,
            device_id=(freq_id, band_id), device_id_type=MESH,
        )

    def peer(s):
        return (zc + s) % chips * 2 + core

    barrier = pltpu.get_barrier_semaphore()
    pl.semaphore_signal(barrier, inc=1, device_id=(f, partner), device_id_type=MESH)
    for s in range(1, chips):
        pl.semaphore_signal(barrier, inc=1, device_id=(f, peer(s)), device_id_type=MESH)
    for s in range(1, groups):
        pl.semaphore_signal(barrier, inc=1, device_id=((f + s) % groups, b), device_id_type=MESH)

    def load(c):
        return pltpu.make_async_copy(
            dens.at[pl.ds(c * piece, piece)], raw.at[pl.ds(c * piece, piece)], sem_in.at[c]
        )

    for c in range(chunks):
        load(c).start()
    pltpu.make_async_copy(trial, both.at[:, pl.ds(pl.multiple_of(core * grid_here, 128), grid_here)], sem_os.at[1]).start()

    def pack(c):
        load(c).wait()
        packed[c] = jnp.swapaxes(raw[c * piece : (c + 1) * piece], 0, 1).reshape(2 * piece, -1)

    def ready():
        pl.semaphore_wait(barrier, chips + groups - 1)

    def waves(c, z):
        return packed.at[c, :, pl.ds(pl.multiple_of(z * wide, 128), wide)]

    sends = []

    def go(copy):
        copy.start()
        sends.append(copy)

    def exchange(c):
        for r in range(1, chips):
            z = (zc + r) % chips
            go(remote(waves(c, z), held.at[c, f, zc], sem_as.at[c, r], sem_ar.at[c, zc], f, peer(r)))

    square_groups = groups == 4
    xx, yy = f % 2, f // 2
    fx, fy = yy * 2 + (1 - xx), (1 - yy) * 2 + xx
    fd = (1 - yy) * 2 + (1 - xx)

    def piece_copy(c, g, z, lane, to):
        ref = held.at[c, g, z]
        return remote(ref, ref, sem_fs.at[c, lane, z], sem_fr.at[c, lane, z], to, b)

    def whole(c, g, lane, to):
        return remote(held.at[c, g], held.at[c, g], sem_fs.at[c, lane, 0], sem_fr.at[c, lane, 0], to, b)

    def own_send(c):
        keep = pltpu.make_async_copy(waves(c, zc), held.at[c, f, zc], sem_ar.at[c, zc])
        keep.start()
        if square_groups:
            for lane, to in ((0, fx), (1, fy)):
                go(remote(waves(c, zc), held.at[c, f, zc], sem_fs.at[c, lane, zc], sem_fr.at[c, lane, zc], to, b))

    def landed(c, z):
        pltpu.make_async_copy(waves(c, 0), held.at[c, f, z], sem_ar.at[c, z]).wait()

    def spread(c, offsets):
        for r in offsets:
            z = (zc + r) % chips
            landed(c, z)
            if square_groups:
                go(piece_copy(c, f, z, 0, fx))
                go(piece_copy(c, f, z, 1, fy))
        if not square_groups and offsets and offsets[-1] == chips - 1:
            landed(c, zc)
            for s in range(1, groups):
                go(whole(c, f, s, (f + s) % groups))

    def relay(c, offsets):
        if square_groups:
            for r in offsets:
                z = (zc + r) % chips
                if (r + c) % 2 == 0:
                    piece_copy(c, fx, z, 0, fx).wait_recv()
                    go(piece_copy(c, fx, z, 2, fy))
                else:
                    piece_copy(c, fy, z, 1, fy).wait_recv()
                    go(piece_copy(c, fy, z, 3, fx))

    def arrive(c):
        if square_groups:
            landed(c, zc)
            for r in range(chips):
                z = (zc + r) % chips
                if (r + c) % 2 == 0:
                    piece_copy(c, fy, z, 1, fy).wait_recv()
                    piece_copy(c, fd, z, 2, fy).wait_recv()
                else:
                    piece_copy(c, fx, z, 0, fx).wait_recv()
                    piece_copy(c, fd, z, 3, fx).wait_recv()
        else:
            for s in range(1, groups):
                src = (f + groups - s) % groups
                whole(c, src, s, src).wait_recv()

    def half_of(ref, k):
        return ref.at[:, pl.ds(pl.multiple_of(k * grid_here, 128), grid_here)]

    def vectors_send():
        go(remote(trial, half_of(both, core), sem_os.at[0], sem_or.at[0], f, partner))

    def vectors():
        pltpu.make_async_copy(trial, half_of(both, core), sem_os.at[1]).wait()
        remote(trial, half_of(both, 1 - core), sem_os.at[0], sem_or.at[0], f, partner).wait_recv()

    def energies():
        cond_count = cond_energy.shape[0]
        val_count = val_energy.shape[0]
        index = pair_index[...]
        rest_index = index
        val_pick = jnp.full(index.shape, val_energy[0], F32)
        for v in range(1, val_count):
            above = index >= v * cond_count
            val_pick = jnp.where(above, val_energy[v], val_pick)
            rest_index = jnp.where(above, index - v * cond_count, rest_index)
        cond_pick = jnp.full(index.shape, cond_energy[0], F32)
        for v in range(1, cond_count):
            cond_pick = jnp.where(rest_index == v, cond_energy[v], cond_pick)
        delta_own[...] = jnp.ones_like(delta_own)
        delta_own[0:1, 0:rows] = cond_pick - val_pick
        for q in range(freqs):
            freq_row[:, q * 2 * vecs : (q + 1) * 2 * vecs] = jnp.full((1, 2 * vecs), frequency[q], F32)
        pltpu.make_async_copy(delta_own, deltas.at[f, zc], sem_dr.at[zc]).start()
        for s in range(1, chips):
            go(remote(delta_own, deltas.at[f, zc], sem_ds.at[s], sem_dr.at[zc], f, peer(s)))

    def pass_deltas():
        for j in range(chips):
            pltpu.make_async_copy(delta_own, deltas.at[f, j], sem_dr.at[j]).wait()
        for s in range(1, groups):
            go(remote(deltas.at[f], deltas.at[f], sem_es.at[s], sem_er.at[s], (f + s) % groups, b))

    def columns():
        for s in range(1, groups):
            src = (f + groups - s) % groups
            remote(deltas.at[src], deltas.at[src], sem_es.at[s], sem_er.at[s], src, b).wait_recv()
        for g in range(groups):
            for j in range(chips):
                turned = jnp.transpose(deltas[g, j])
                at = (g * chips + j) * piece
                for c in range(chunks):
                    cols[c, at : at + piece, :] = turned[c * piece : (c + 1) * piece, :]

    hw = width // 2

    def weights(column, h):
        freq = freq_row[:, h * hw : (h + 1) * hw]
        ratio = column / (column * column + freq * freq)
        return (-4.0 * prefactor * ratio).astype(BF16).astype(F32)

    lane_at = lax.broadcasted_iota(jnp.int32, (1, 2 * vecs), 1)

    def swap(x, low, high):
        sign = jnp.where(lane_at < vecs, low, high)
        return jnp.concatenate(
            [
                pltpu.roll(x[:, q * 2 * vecs : (q + 1) * 2 * vecs], vecs, 1) * sign
                for q in range(freqs // 2)
            ],
            axis=1,
        )

    def cross(j, h):
        if h == 0:
            arrive(j)
        over_grid = (((1,), (1,)), ((), ()))
        out = lax.dot_general(
            held[j].reshape(2 * chunk_rows, wide),
            both[h * hw : (h + 1) * hw, :],
            over_grid,
            preferred_element_type=F32,
        ).reshape(groups * chips, 2, piece, hw)
        total = out[:, 0].reshape(chunk_rows, hw) + swap(
            out[:, 1].reshape(chunk_rows, hw), 1.0, -1.0
        )
        ring_out[j, h] = total.astype(BF16).reshape(chips, slot, hw)
        if split(j) or h == 1:
            for s in range(1, chips):
                go(slot_copy(j, h, s, (zc + s) % chips))

    def split(j):
        return j == chunks - 1

    def slot_copy(j, h, s, at):
        if split(j):
            src, dst = ring_out.at[j, h, at], ring_in.at[j, h, s]
        else:
            src, dst, h = ring_out.at[j, :, at], ring_in.at[j, :, s], 0
        return remote(src, dst, sem_rs.at[j, h, s], sem_rr.at[j, h, s], f, peer(s))

    def scaled_copy(j, h, s, at):
        if split(j):
            ref = scaled.at[j, h, at]
        else:
            ref, h = scaled.at[j, :, at], 0
        return remote(ref, ref, sem_gs.at[j, h, s], sem_gr.at[j, h, s], f, peer(s))

    def scale(j, h):
        total = ring_out[j, h, zc].astype(F32)
        for s in range(1, chips):
            if split(j) or h == 0:
                slot_copy(j, h, s, zc).wait_recv()
            total = total + ring_in[j, h, s].astype(F32)
        column = cols[j, pl.ds(pl.multiple_of(zc * slot, 8), slot), 0:1]
        scaled[j, h, zc] = (weights(column, h) * total).astype(BF16)
        if split(j) or h == 1:
            for s in range(1, chips):
                go(scaled_copy(j, h, s, zc))

    def share(j, h):
        if split(j) or h == 0:
            for s in range(1, chips):
                scaled_copy(j, h, s, (zc + chips - s) % chips).wait_recv()

    over_rows = (((0,), (0,)), ((), ()))

    def paired(j, h):
        flat32 = scaled[j, h].reshape(chunk_rows, hw).astype(F32)
        turned = swap(flat32, -1.0, 1.0)
        return jnp.concatenate(
            [
                flat32.reshape(groups * chips, 1, piece, hw),
                turned.reshape(groups * chips, 1, piece, hw),
            ],
            axis=1,
        ).reshape(2 * chunk_rows, hw).astype(BF16)

    def term(j, left, k):
        right = held[j, :, :, :, pl.ds(pl.multiple_of(k * grid_here, 128), grid_here)]
        return lax.dot_general(
            left, right.reshape(2 * chunk_rows, grid_here), over_rows, preferred_element_type=F32
        )

    def squares(j, h):
        flat = scaled[j, h].reshape(chunk_rows, hw)
        column = cols[j, :, 0:1]
        crossing = (flat.astype(F32) / weights(column, h)).astype(BF16)
        for i in range(freqs // 2):
            lo, hi = i * 2 * vecs, (i + 1) * 2 * vecs
            q = h * (freqs // 2) + i
            square = lax.dot_general(
                crossing[:, lo:hi], flat[:, lo:hi], over_rows, preferred_element_type=F32
            )
            if j == 0:
                acc[q] = square
            else:
                acc[q] = acc[q] + square

    def image(j, h):
        left = paired(j, h)
        part = slice(h * hw, (h + 1) * hw)
        if j == 0:
            other[part, :] = term(j, left, 1 - core)
            total_own[part, :] = term(j, left, core)
        else:
            other[part, :] = other[part, :] + term(j, left, 1 - core)
            total_own[part, :] = total_own[part, :] + term(j, left, core)
        squares(j, h)

    quarter = width // 4

    def late_copy(k):
        part = pl.ds(k * quarter, quarter)
        return remote(late_out.at[part], late_in.at[part], sem_is.at[k], sem_ir.at[k], f, partner)

    def sub_copy():
        return remote(sub_out, sub_in, sem_is.at[4], sem_ir.at[4], f, partner)

    def last_other(h):
        j = chunks - 1
        left = paired(j, h)
        for i in range(2):
            k = 2 * h + i
            part = slice(k * quarter, (k + 1) * quarter)
            late_out[part, :] = (
                other[part, :] + term(j, left[:, i * quarter : (i + 1) * quarter], 1 - core)
            ).astype(BF16)
            go(late_copy(k))
        part = slice(h * hw, (h + 1) * hw)
        total_own[part, :] = total_own[part, :] + term(j, left, core)
        squares(j, h)

    def last_sub():
        for q in range(freqs):
            square = acc[q]
            lo, hi = q * 2 * vecs, (q * 2 + 1) * vecs
            sub_out[lo : lo + vecs, :] = (square[0:vecs, 0:vecs] + square[vecs:, vecs:]) * inv_grid
            sub_out[hi : hi + vecs, :] = (square[0:vecs, vecs:] - square[vecs:, 0:vecs]) * inv_grid
        go(sub_copy())

    def store(k):
        part = pl.ds(k * quarter, quarter)
        return pltpu.make_async_copy(total_own.at[part], images.at[part], sem_out.at[k])

    def last_add(k):
        late_copy(k).wait_recv()
        part = slice(k * quarter, (k + 1) * quarter)
        total_own[part, :] = total_own[part, :] + late_in[part, :].astype(F32)
        store(k).start()

    def last_wait():
        sub_copy().wait_recv()
        sub[...] = sub_out[...] + sub_in[...]
        for k in range(4):
            store(k).wait()

    one, two, rest = (1,), range(2, 3), range(3, chips)
    own = (0,)
    pack(0)
    pack(1)
    pack(2)
    pack(3)
    ready()
    exchange(0)
    for c in range(chunks):
        own_send(c)
    energies()
    vectors_send()
    relay(0, own)
    relay(1, own)
    spread(0, one)
    exchange(1)
    relay(2, own)
    spread(0, two)
    relay(3, own)
    spread(0, rest)
    relay(0, one)
    spread(1, one)
    relay(0, two)
    spread(1, two)
    exchange(2)
    relay(0, rest)
    spread(1, rest)
    pass_deltas()
    vectors()
    relay(1, one)
    spread(2, one)
    relay(1, two)
    spread(2, two)
    exchange(3)
    cross(0, 0)
    cross(0, 1)
    relay(1, rest)
    spread(2, rest)
    relay(2, one)
    spread(3, one)
    relay(2, two)
    spread(3, two)
    relay(2, rest)
    spread(3, rest)
    cross(1, 0)
    cross(1, 1)
    columns()
    scale(0, 0)
    scale(0, 1)
    relay(3, one)
    relay(3, two)
    cross(2, 0)
    cross(2, 1)
    relay(3, rest)
    scale(1, 0)
    scale(1, 1)
    share(0, 0)
    image(0, 0)
    image(0, 1)
    cross(3, 0)
    cross(3, 1)
    scale(2, 0)
    scale(2, 1)
    share(1, 0)
    image(1, 0)
    image(1, 1)
    scale(3, 0)
    scale(3, 1)
    share(2, 0)
    image(2, 0)
    image(2, 1)
    share(3, 0)
    last_other(0)
    share(3, 1)
    last_other(1)
    last_sub()
    last_add(0)
    last_add(1)
    last_add(2)
    last_add(3)
    last_wait()
    for copy in sends:
        copy.wait_send()


def shards(pair_density, trial_vectors, frequency, val_energy, cond_energy, pair_index):
    groups = lax.axis_size("freq")
    members = lax.axis_size("band")
    rows = pair_density.shape[0]
    freqs, _, vecs, grid_here = trial_vectors.shape
    pair_count = rows * groups * members
    grid_count = grid_here * members
    prefactor = 1.0 / math.sqrt(2.0 * grid_count * pair_count)
    width = freqs * 2 * vecs
    chips = members // 2
    chunks = rows // 8
    piece = rows // chunks
    slot = groups * piece
    wide = 2 * grid_here
    trial = trial_vectors.reshape(width, grid_here)
    dma = pltpu.SemaphoreType.DMA
    vmem = pl.BlockSpec(memory_space=pltpu.VMEM)
    anywhere = pl.BlockSpec(memory_space=pl.ANY)
    smem = pl.BlockSpec(memory_space=pltpu.SMEM)
    images, sub = pl.pallas_call(
        functools.partial(
            kernel, groups, members, chunks, freqs, vecs, rows, grid_here, prefactor, 1.0 / grid_count
        ),
        out_shape=(
            jax.ShapeDtypeStruct((width, grid_here), F32),
            jax.ShapeDtypeStruct((width, vecs), F32),
        ),
        in_specs=[anywhere] * 2 + [smem] * 3 + [vmem],
        out_specs=(anywhere, vmem),
        scratch_shapes=[
            pltpu.VMEM((rows, 2, grid_count), BF16),
            pltpu.VMEM((chunks, 2 * piece, grid_count), BF16),
            pltpu.VMEM((width, grid_here), F32),
            pltpu.VMEM((chunks, groups, chips, 2 * piece, wide), BF16),
            pltpu.VMEM((width, wide), BF16),
            pltpu.VMEM((8, 128), F32),
            pltpu.VMEM((1, width), F32),
            pltpu.VMEM((groups, chips, 8, 128), F32),
            pltpu.VMEM((chunks, chips * slot, 8), F32),
            pltpu.VMEM((chunks, 2, chips, slot, width // 2), BF16),
            pltpu.VMEM((chunks, 2, chips, slot, width // 2), BF16),
            pltpu.VMEM((chunks, 2, chips, slot, width // 2), BF16),
            pltpu.VMEM((freqs, 2 * vecs, 2 * vecs), F32),
            pltpu.VMEM((width, grid_here), F32),
            pltpu.VMEM((width, grid_here), BF16),
            pltpu.VMEM((width, grid_here), BF16),
            pltpu.VMEM((width, vecs), F32),
            pltpu.VMEM((width, vecs), F32),
            dma((chunks,)), dma((4,)),
            dma((chunks, chips)), dma((chunks, chips)),
            dma((2,)), dma((1,)),
            dma((chunks, groups, chips)), dma((chunks, groups, chips)),
            dma((chips,)), dma((chips,)),
            dma((groups,)), dma((groups,)),
            dma((chunks, 2, chips)), dma((chunks, 2, chips)),
            dma((chunks, 2, chips)), dma((chunks, 2, chips)),
            dma((5,)), dma((5,)),
        ],
        compiler_params=pltpu.CompilerParams(
            collective_id=0, has_side_effects=True, vmem_limit_bytes=56 * 1024 * 1024
        ),
    )(pair_density, trial, frequency, val_energy, cond_energy, pair_index[None, :])
    return (
        images.reshape(freqs, 2, vecs, grid_here),
        sub.reshape(freqs, 2, vecs, vecs),
    )


def solution(mesh):
    return jax.shard_map(
        shards,
        mesh=mesh,
        in_specs=(
            P(("freq", "band"), None, None),
            P("freq", None, None, "band"),
            P("freq"),
            P(),
            P(),
            P(("freq", "band")),
        ),
        out_specs=(P("freq", None, None, "band"), P("freq", None, None, None)),
        check_vma=False,
    )
```

time: 78.6 us -> 67.5 us (0.86)
  Pallas kernels: 71 us -> 62.5 us
  local copies, waits for them, and re-layouts: 6.68 us -> 3.91 us
    pallas_call x1, Pallas kernels: 71 us -> 62.5 us  [shards(): pl.pallas_call(functools.partial(kernel, groups, members, chunks, freqs,...]
    reshape x1 -> x0, local copies, waits for them, and re-layouts: 2.78 us -> none  [shards(): pair_density.reshape(chunks, piece, 2, grid_count)]
where the time goes in v1:
time: 67.5 us; the launch traced here: 67.1 us
  Pallas kernels  62.5 us (93%)
  local copies, waits for them, and re-layouts  3.91 us (6%)
    pallas_call x1, Pallas kernels, shards(): pl.pallas_call(functools.partial(kernel, groups, members, chunks, freqs,...  62.5 us
    unnamed x4, local copies, waits for them, and re-layouts  3.91 us

profile of v1, /device:TPU:3, one launch (start us, length us, event | category | flops | bytes accessed | tf_op | source)
XLA Modules:
  0.0 67.1 jit_solution(14550041158379077793)
XLA Ops:
  0.6 62.5 %shard_map.77 = (f32[512,1024]{1,0:T(8,128)}, f32[512,64]{1,0:T(8,128)}) custom-call(bf16[32,2,8192]{2,1,0:T(2,128)(2,1)} %dens.1, bf16[512,1024]{1,0:T(8,128)(2,1)} %bitcast.5, f32[4]{0:T(128)} %frequency.1, f32[32]{0:T(128)} %val_energy.1, f32[32]{0:T(128)} %cond_energy.1, s32[1,32]{1,0:T(1,128)} %bitcast.7), custom_call_target="tpu_custom_call" | custom-call | tf_op jit(solution)/shard_map/pallas_call | solution.py:459
  63.2 0.0 copy-start
  63.2 3.2 %copy.10 = f32[4,2,64,1024]{3,2,1,0:T(8,128)} copy(f32[4,2,64,1024]{3,2,1,0:T(8,128)} %bitcast.4) | data formatting | bytes 4194304
  66.4 0.0 copy-done
  66.4 0.7 %copy.11 = f32[4,2,64,64]{3,2,1,0:T(8,128)} copy(f32[4,2,64,64]{3,2,1,0:T(8,128)S(1)} %bitcast.6) | data formatting | bytes 262144
Async XLA Ops:
  63.2 3.2 %copy-start = (f32[512,64]{1,0:T(8,128)S(1)}, f32[512,64]{1,0:T(8,128)}, u32[]{:S(2)}) copy-start(f32[512,64]{1,0:T(8,128)} %get-tuple-element.5) | copy-start | bytes 393220

commit v2 on v1

--- a/solution.py
+++ b/solution.py
@@ -13,14 +13,15 @@
 BF16 = jnp.bfloat16
 
 
-def kernel(
+def scoped(
     groups, members, chunks, freqs, vecs, rows, grid_here, prefactor, inv_grid,
-    dens, trial, frequency, val_energy, cond_energy, pair_index,
-    images, sub,
+    dens, trial, frequency_in, val_in, cond_in, index_in,
+    total_out, sub_mine, sub_in,
+    frequency, val_energy, cond_energy, pair_index,
     raw, packed, total_own, held, both, delta_own, freq_row, deltas, cols, ring_out, ring_in, scaled, acc,
-    other, late_out, late_in, sub_out, sub_in,
+    sub_out, held_p, scaled_p,
     sem_in, sem_out, sem_as, sem_ar, sem_os, sem_or, sem_fs, sem_fr, sem_ds, sem_dr, sem_es, sem_er,
-    sem_rs, sem_rr, sem_gs, sem_gr, sem_is, sem_ir,
+    sem_rs, sem_rr, sem_gs, sem_gr, sem_ls, sem_lr, sem_qs, sem_qr, sem_is, sem_ir,
 ):
     f = lax.axis_index("freq")
     b = lax.axis_index("band")
@@ -57,6 +58,14 @@
 
     for c in range(chunks):
         load(c).start()
+    small = [
+        pltpu.make_async_copy(src, dst, sem_in.at[chunks + i])
+        for i, (src, dst) in enumerate(
+            ((frequency_in, frequency), (val_in, val_energy), (cond_in, cond_energy), (index_in, pair_index))
+        )
+    ]
+    for copy in small:
+        copy.start()
     pltpu.make_async_copy(trial, both.at[:, pl.ds(pl.multiple_of(core * grid_here, 128), grid_here)], sem_os.at[1]).start()
 
     def pack(c):
@@ -152,6 +161,8 @@
         remote(trial, half_of(both, 1 - core), sem_os.at[0], sem_or.at[0], f, partner).wait_recv()
 
     def energies():
+        for copy in small:
+            copy.wait()
         cond_count = cond_energy.shape[0]
         val_count = val_energy.shape[0]
         index = pair_index[...]
@@ -208,23 +219,35 @@
             axis=1,
         )
 
-    def cross(j, h):
-        if h == 0:
-            arrive(j)
+    def lend(j):
+        return remote(
+            held.at[j, :, :, :, pl.ds(pl.multiple_of((1 - core) * grid_here, 128), grid_here)],
+            held_p.at[j], sem_ls.at[j], sem_lr.at[j], f, partner,
+        )
+
+    def scaled_lend(j, h):
+        if split(j):
+            src, dst = scaled.at[j, h], scaled_p.at[j, h]
+        else:
+            src, dst, h = scaled.at[j], scaled_p.at[j], 0
+        return remote(src, dst, sem_qs.at[j, h], sem_qr.at[j, h], f, partner)
+
+    def cross(j):
+        arrive(j)
+        go(lend(j))
         over_grid = (((1,), (1,)), ((), ()))
         out = lax.dot_general(
-            held[j].reshape(2 * chunk_rows, wide),
-            both[h * hw : (h + 1) * hw, :],
-            over_grid,
-            preferred_element_type=F32,
-        ).reshape(groups * chips, 2, piece, hw)
-        total = out[:, 0].reshape(chunk_rows, hw) + swap(
-            out[:, 1].reshape(chunk_rows, hw), 1.0, -1.0
-        )
-        ring_out[j, h] = total.astype(BF16).reshape(chips, slot, hw)
-        if split(j) or h == 1:
-            for s in range(1, chips):
-                go(slot_copy(j, h, s, (zc + s) % chips))
+            held[j].reshape(2 * chunk_rows, wide), both[...], over_grid, preferred_element_type=F32
+        ).reshape(groups * chips, 2, piece, width)
+        for h in range(2):
+            part = slice(h * hw, (h + 1) * hw)
+            total = out[:, 0, :, part].reshape(chunk_rows, hw) + swap(
+                out[:, 1, :, part].reshape(chunk_rows, hw), 1.0, -1.0
+            )
+            ring_out[j, h] = total.astype(BF16).reshape(chips, slot, hw)
+            if split(j) or h == 1:
+                for s in range(1, chips):
+                    go(slot_copy(j, h, s, (zc + s) % chips))
 
     def split(j):
         return j == chunks - 1
@@ -259,11 +282,12 @@
         if split(j) or h == 0:
             for s in range(1, chips):
                 scaled_copy(j, h, s, (zc + chips - s) % chips).wait_recv()
+            go(scaled_lend(j, h))
 
     over_rows = (((0,), (0,)), ((), ()))
 
-    def paired(j, h):
-        flat32 = scaled[j, h].reshape(chunk_rows, hw).astype(F32)
+    def paired(block):
+        flat32 = block.reshape(chunk_rows, hw).astype(F32)
         turned = swap(flat32, -1.0, 1.0)
         return jnp.concatenate(
             [
@@ -273,10 +297,32 @@
             axis=1,
         ).reshape(2 * chunk_rows, hw).astype(BF16)
 
-    def term(j, left, k):
-        right = held[j, :, :, :, pl.ds(pl.multiple_of(k * grid_here, 128), grid_here)]
+    def add(j, h, term):
+        part = slice(h * hw, (h + 1) * hw)
+        if j == 0:
+            total_own[part, :] = term
+        else:
+            total_own[part, :] = total_own[part, :] + term
+
+    def here(j, h):
+        right = held[j, :, :, :, pl.ds(pl.multiple_of(core * grid_here, 128), grid_here)]
         return lax.dot_general(
-            left, right.reshape(2 * chunk_rows, grid_here), over_rows, preferred_element_type=F32
+            paired(scaled[j, h]),
+            right.reshape(2 * chunk_rows, grid_here),
+            over_rows,
+            preferred_element_type=F32,
+        )
+
+    def lent(j, h):
+        if h == 0:
+            lend(j).wait_recv()
+        if split(j) or h == 0:
+            scaled_lend(j, h).wait_recv()
+        return lax.dot_general(
+            paired(scaled_p[j, h]),
+            held_p[j].reshape(2 * chunk_rows, grid_here),
+            over_rows,
+            preferred_element_type=F32,
         )
 
     def squares(j, h):
@@ -295,38 +341,20 @@
                 acc[q] = acc[q] + square
 
     def image(j, h):
-        left = paired(j, h)
-        part = slice(h * hw, (h + 1) * hw)
-        if j == 0:
-            other[part, :] = term(j, left, 1 - core)
-            total_own[part, :] = term(j, left, core)
-        else:
-            other[part, :] = other[part, :] + term(j, left, 1 - core)
-            total_own[part, :] = total_own[part, :] + term(j, left, core)
-        squares(j, h)
-
-    quarter = width // 4
-
-    def late_copy(k):
-        part = pl.ds(k * quarter, quarter)
-        return remote(late_out.at[part], late_in.at[part], sem_is.at[k], sem_ir.at[k], f, partner)
+        add(j, h, here(j, h) + lent(j, h))
+
+    def last_own(h):
+        add(chunks - 1, h, here(chunks - 1, h))
+
+    def last_lent(h):
+        add(chunks - 1, h, lent(chunks - 1, h))
+        store(h).start()
 
     def sub_copy():
-        return remote(sub_out, sub_in, sem_is.at[4], sem_ir.at[4], f, partner)
-
-    def last_other(h):
-        j = chunks - 1
-        left = paired(j, h)
-        for i in range(2):
-            k = 2 * h + i
-            part = slice(k * quarter, (k + 1) * quarter)
-            late_out[part, :] = (
-                other[part, :] + term(j, left[:, i * quarter : (i + 1) * quarter], 1 - core)
-            ).astype(BF16)
-            go(late_copy(k))
-        part = slice(h * hw, (h + 1) * hw)
-        total_own[part, :] = total_own[part, :] + term(j, left, core)
-        squares(j, h)
+        return remote(sub_out, sub_in, sem_is.at[0], sem_ir.at[0], f, partner)
+
+    def sub_keep():
+        return pltpu.make_async_copy(sub_out, sub_mine, sem_out.at[2])
 
     def last_sub():
         for q in range(freqs):
@@ -335,22 +363,17 @@
             sub_out[lo : lo + vecs, :] = (square[0:vecs, 0:vecs] + square[vecs:, vecs:]) * inv_grid
             sub_out[hi : hi + vecs, :] = (square[0:vecs, vecs:] - square[vecs:, 0:vecs]) * inv_grid
         go(sub_copy())
-
-    def store(k):
-        part = pl.ds(k * quarter, quarter)
-        return pltpu.make_async_copy(total_own.at[part], images.at[part], sem_out.at[k])
-
-    def last_add(k):
-        late_copy(k).wait_recv()
-        part = slice(k * quarter, (k + 1) * quarter)
-        total_own[part, :] = total_own[part, :] + late_in[part, :].astype(F32)
-        store(k).start()
+        sub_keep().start()
+
+    def store(h):
+        part = pl.ds(h * hw, hw)
+        return pltpu.make_async_copy(total_own.at[part], total_out.at[part], sem_out.at[h])
 
     def last_wait():
+        for h in range(2):
+            store(h).wait()
+        sub_keep().wait()
         sub_copy().wait_recv()
-        sub[...] = sub_out[...] + sub_in[...]
-        for k in range(4):
-            store(k).wait()
 
     one, two, rest = (1,), range(2, 3), range(3, chips)
     own = (0,)
@@ -386,8 +409,7 @@
     relay(1, two)
     spread(2, two)
     exchange(3)
-    cross(0, 0)
-    cross(0, 1)
+    cross(0)
     relay(1, rest)
     spread(2, rest)
     relay(2, one)
@@ -396,45 +418,85 @@
     spread(3, two)
     relay(2, rest)
     spread(3, rest)
-    cross(1, 0)
-    cross(1, 1)
+    cross(1)
     columns()
     scale(0, 0)
     scale(0, 1)
     relay(3, one)
     relay(3, two)
-    cross(2, 0)
-    cross(2, 1)
+    cross(2)
     relay(3, rest)
     scale(1, 0)
     scale(1, 1)
     share(0, 0)
+    squares(0, 0)
+    squares(0, 1)
+    cross(3)
+    scale(2, 0)
+    scale(2, 1)
     image(0, 0)
     image(0, 1)
-    cross(3, 0)
-    cross(3, 1)
-    scale(2, 0)
-    scale(2, 1)
     share(1, 0)
+    squares(1, 0)
+    squares(1, 1)
+    scale(3, 0)
+    scale(3, 1)
     image(1, 0)
     image(1, 1)
-    scale(3, 0)
-    scale(3, 1)
     share(2, 0)
+    squares(2, 0)
+    squares(2, 1)
     image(2, 0)
     image(2, 1)
     share(3, 0)
-    last_other(0)
+    last_own(0)
+    squares(3, 0)
     share(3, 1)
-    last_other(1)
+    squares(3, 1)
     last_sub()
-    last_add(0)
-    last_add(1)
-    last_add(2)
-    last_add(3)
+    last_own(1)
+    last_lent(0)
+    last_lent(1)
     last_wait()
     for copy in sends:
         copy.wait_send()
+
+
+def kernel(statics, semaphores, *refs):
+    pl.run_scoped(functools.partial(scoped, *statics, *refs), *semaphores)
+
+
+def closing(total, sub_mine, sub_in, images, sub, total_v, sub_v, sub_iv, sem_a, sem_b, sem_c):
+    blocks = sem_c.shape[0] - 1
+    size = total.shape[0] // blocks
+
+    def into(k):
+        part = pl.ds(k * size, size)
+        return pltpu.make_async_copy(total.at[part], total_v.at[part], sem_a.at[k])
+
+    def out(k):
+        part = pl.ds(k * size, size)
+        return pltpu.make_async_copy(total_v.at[part], images.at[part], sem_c.at[k])
+
+    for k in range(blocks):
+        into(k).start()
+    edge = (
+        pltpu.make_async_copy(sub_mine, sub_v, sem_b.at[0]),
+        pltpu.make_async_copy(sub_in, sub_iv, sem_b.at[1]),
+    )
+    for copy in edge:
+        copy.start()
+    for k in range(blocks):
+        into(k).wait()
+        out(k).start()
+    for copy in edge:
+        copy.wait()
+    sub_v[...] = sub_v[...] + sub_iv[...]
+    last = pltpu.make_async_copy(sub_v, sub, sem_c.at[blocks])
+    last.start()
+    for k in range(blocks):
+        out(k).wait()
+    last.wait()
 
 
 def shards(pair_density, trial_vectors, frequency, val_energy, cond_energy, pair_index):
@@ -453,20 +515,25 @@
     wide = 2 * grid_here
     trial = trial_vectors.reshape(width, grid_here)
     dma = pltpu.SemaphoreType.DMA
-    vmem = pl.BlockSpec(memory_space=pltpu.VMEM)
     anywhere = pl.BlockSpec(memory_space=pl.ANY)
-    smem = pl.BlockSpec(memory_space=pltpu.SMEM)
-    images, sub = pl.pallas_call(
-        functools.partial(
-            kernel, groups, members, chunks, freqs, vecs, rows, grid_here, prefactor, 1.0 / grid_count
-        ),
+    statics = (groups, members, chunks, freqs, vecs, rows, grid_here, prefactor, 1.0 / grid_count)
+    semaphores = (
+        dma((chunks + 4,)), dma((3,)), dma((chunks, chips)), dma((chunks, chips)), dma((2,)), dma((1,)), dma((chunks, groups, chips)), dma((chunks, groups, chips)), dma((chips,)), dma((chips,)), dma((groups,)), dma((groups,)), dma((chunks, 2, chips)), dma((chunks, 2, chips)), dma((chunks, 2, chips)), dma((chunks, 2, chips)), dma((chunks,)), dma((chunks,)), dma((chunks, 2)), dma((chunks, 2)), dma((1,)), dma((1,)),
+    )
+    parts = pl.pallas_call(
+        functools.partial(kernel, statics, semaphores),
         out_shape=(
             jax.ShapeDtypeStruct((width, grid_here), F32),
             jax.ShapeDtypeStruct((width, vecs), F32),
+            jax.ShapeDtypeStruct((width, vecs), F32),
         ),
-        in_specs=[anywhere] * 2 + [smem] * 3 + [vmem],
-        out_specs=(anywhere, vmem),
+        in_specs=[anywhere] * 6,
+        out_specs=(anywhere,) * 3,
         scratch_shapes=[
+            pltpu.SMEM(frequency.shape, F32),
+            pltpu.SMEM(val_energy.shape, F32),
+            pltpu.SMEM(cond_energy.shape, F32),
+            pltpu.VMEM((1, rows), jnp.int32),
             pltpu.VMEM((rows, 2, grid_count), BF16),
             pltpu.VMEM((chunks, 2 * piece, grid_count), BF16),
             pltpu.VMEM((width, grid_here), F32),
@@ -480,25 +547,30 @@
             pltpu.VMEM((chunks, 2, chips, slot, width // 2), BF16),
             pltpu.VMEM((chunks, 2, chips, slot, width // 2), BF16),
             pltpu.VMEM((freqs, 2 * vecs, 2 * vecs), F32),
-            pltpu.VMEM((width, grid_here), F32),
-            pltpu.VMEM((width, grid_here), BF16),
-            pltpu.VMEM((width, grid_here), BF16),
             pltpu.VMEM((width, vecs), F32),
-            pltpu.VMEM((width, vecs), F32),
-            dma((chunks,)), dma((4,)),
-            dma((chunks, chips)), dma((chunks, chips)),
-            dma((2,)), dma((1,)),
-            dma((chunks, groups, chips)), dma((chunks, groups, chips)),
-            dma((chips,)), dma((chips,)),
-            dma((groups,)), dma((groups,)),
-            dma((chunks, 2, chips)), dma((chunks, 2, chips)),
-            dma((chunks, 2, chips)), dma((chunks, 2, chips)),
-            dma((5,)), dma((5,)),
+            pltpu.VMEM((chunks, groups, chips, 2 * piece, grid_here), BF16),
+            pltpu.VMEM((chunks, 2, chips, slot, width // 2), BF16),
         ],
         compiler_params=pltpu.CompilerParams(
             collective_id=0, has_side_effects=True, vmem_limit_bytes=56 * 1024 * 1024
         ),
     )(pair_density, trial, frequency, val_energy, cond_energy, pair_index[None, :])
+    blocks = 4
+    images, sub = pl.pallas_call(
+        closing,
+        out_shape=(
+            jax.ShapeDtypeStruct((width, grid_here), F32),
+            jax.ShapeDtypeStruct((width, vecs), F32),
+        ),
+        in_specs=[anywhere] * 3,
+        out_specs=(anywhere,) * 2,
+        scratch_shapes=[
+            pltpu.VMEM((width, grid_here), F32),
+            pltpu.VMEM((width, vecs), F32),
+            pltpu.VMEM((width, vecs), F32),
+            dma((blocks,)), dma((2,)), dma((blocks + 1,)),
+        ],
+    )(*parts)
     return (
         images.reshape(freqs, 2, vecs, grid_here),
         sub.reshape(freqs, 2, vecs, vecs),

time: 67.5 us -> 61.9 us (0.917)
  local copies, waits for them, and re-layouts: 3.91 us -> 0 us
  Pallas kernels: 62.5 us -> 60.2 us
    unnamed x4 -> x0, local copies, waits for them, and re-layouts: 3.91 us -> none
    pallas_call x1 -> x2, Pallas kernels: 62.5 us -> 60.2 us  [the longest x1 57.6 us: shards(): pl.pallas_call(functools.partial(kernel, statics, semaphores), out_shape=...]
where the time goes in v2:
time: 61.9 us; the launch traced here: 60.8 us
  Pallas kernels  60.2 us (97%)
  between operations  0.64 us (1%)
    pallas_call x1, Pallas kernels, shards(): pl.pallas_call(functools.partial(kernel, statics, semaphores), out_shape=...  57.6 us
    pallas_call x1, Pallas kernels, shards(): pl.pallas_call(closing, out_shape=(jax.ShapeDtypeStruct((width, grid_here...  2.57 us

profile of v2, /device:TPU:3, one launch (start us, length us, event | category | flops | bytes accessed | tf_op | source)
XLA Modules:
  0.0 60.8 jit_solution(12727325874835790829)
XLA Ops:
  0.6 57.6 %shard_map.77 = (f32[512,1024]{1,0:T(8,128)}, f32[512,64]{1,0:T(8,128)}, f32[512,64]{1,0:T(8,128)}) custom-call(bf16[32,2,8192]{2,1,0:T(2,128)(2,1)} %refs_0_.1, bf16[512,1024]{1,0:T(8,128)(2,1)} %bitcast.4, f32[4]{0:T(128)} %refs_2_.1, f32[32]{0:T(128)} %refs_3_.1, f32[32]{0:T(128)} %refs_4_.1, s32[1,32]{1,0:T(1,128)} %bitcast.5), custom_call_target="tpu_custom_call" | custom-call | tf_op jit(solution)/shard_map/pallas_call | solution.py:523
  58.3 2.6 %shard_map.78 = (f32[512,1024]{1,0:T(8,128)}, f32[512,64]{1,0:T(8,128)}) custom-call(f32[512,1024]{1,0:T(8,128)} %get-tuple-element.7.total, f32[512,64]{1,0:T(8,128)} %get-tuple-element.8.sub_mine, f32[512,64]{1,0:T(8,128)} %get-tuple-element.9.sub_in), custom_call_target="tpu_custom_call" | custom-call | tf_op jit(solution)/shard_map/pallas_call | solution.py:559

commit v3 on v2

--- a/solution.py
+++ b/solution.py
@@ -16,11 +16,11 @@
 def scoped(
     groups, members, chunks, freqs, vecs, rows, grid_here, prefactor, inv_grid,
     dens, trial, frequency_in, val_in, cond_in, index_in,
-    total_out, sub_mine, sub_in,
+    total_own, sub_out, sub_in,
     frequency, val_energy, cond_energy, pair_index,
-    raw, packed, total_own, held, both, delta_own, freq_row, deltas, cols, ring_out, ring_in, scaled, acc,
-    sub_out, held_p, scaled_p,
-    sem_in, sem_out, sem_as, sem_ar, sem_os, sem_or, sem_fs, sem_fr, sem_ds, sem_dr, sem_es, sem_er,
+    raw, packed, held, both, delta_own, freq_row, deltas, cols, ring_out, ring_in, scaled, acc,
+    held_p, scaled_p,
+    sem_in, sem_as, sem_ar, sem_os, sem_or, sem_fs, sem_fr, sem_ds, sem_dr, sem_es, sem_er,
     sem_rs, sem_rr, sem_gs, sem_gr, sem_ls, sem_lr, sem_qs, sem_qr, sem_is, sem_ir,
 ):
     f = lax.axis_index("freq")
@@ -348,13 +348,9 @@
 
     def last_lent(h):
         add(chunks - 1, h, lent(chunks - 1, h))
-        store(h).start()
 
     def sub_copy():
         return remote(sub_out, sub_in, sem_is.at[0], sem_ir.at[0], f, partner)
-
-    def sub_keep():
-        return pltpu.make_async_copy(sub_out, sub_mine, sem_out.at[2])
 
     def last_sub():
         for q in range(freqs):
@@ -363,16 +359,8 @@
             sub_out[lo : lo + vecs, :] = (square[0:vecs, 0:vecs] + square[vecs:, vecs:]) * inv_grid
             sub_out[hi : hi + vecs, :] = (square[0:vecs, vecs:] - square[vecs:, 0:vecs]) * inv_grid
         go(sub_copy())
-        sub_keep().start()
-
-    def store(h):
-        part = pl.ds(h * hw, hw)
-        return pltpu.make_async_copy(total_own.at[part], total_out.at[part], sem_out.at[h])
 
     def last_wait():
-        for h in range(2):
-            store(h).wait()
-        sub_keep().wait()
         sub_copy().wait_recv()
 
     one, two, rest = (1,), range(2, 3), range(3, chips)
@@ -405,8 +393,8 @@
     pass_deltas()
     vectors()
     relay(1, one)
+    relay(1, two)
     spread(2, one)
-    relay(1, two)
     spread(2, two)
     exchange(3)
     cross(0)
@@ -417,20 +405,20 @@
     relay(2, two)
     spread(3, two)
     relay(2, rest)
+    columns()
     spread(3, rest)
     cross(1)
-    columns()
     scale(0, 0)
     scale(0, 1)
     relay(3, one)
     relay(3, two)
     cross(2)
-    relay(3, rest)
     scale(1, 0)
     scale(1, 1)
     share(0, 0)
     squares(0, 0)
     squares(0, 1)
+    relay(3, rest)
     cross(3)
     scale(2, 0)
     scale(2, 1)
@@ -466,37 +454,17 @@
     pl.run_scoped(functools.partial(scoped, *statics, *refs), *semaphores)
 
 
-def closing(total, sub_mine, sub_in, images, sub, total_v, sub_v, sub_iv, sem_a, sem_b, sem_c):
-    blocks = sem_c.shape[0] - 1
-    size = total.shape[0] // blocks
-
-    def into(k):
-        part = pl.ds(k * size, size)
-        return pltpu.make_async_copy(total.at[part], total_v.at[part], sem_a.at[k])
-
-    def out(k):
-        part = pl.ds(k * size, size)
-        return pltpu.make_async_copy(total_v.at[part], images.at[part], sem_c.at[k])
-
-    for k in range(blocks):
-        into(k).start()
-    edge = (
-        pltpu.make_async_copy(sub_mine, sub_v, sem_b.at[0]),
-        pltpu.make_async_copy(sub_in, sub_iv, sem_b.at[1]),
-    )
-    for copy in edge:
+def closing(total, sub_mine, sub_in, images, sub, sub_v):
+    def run(sem):
+        copy = pltpu.make_async_copy(total, images, sem.at[0])
         copy.start()
-    for k in range(blocks):
-        into(k).wait()
-        out(k).start()
-    for copy in edge:
+        sub_v[...] = sub_mine[...] + sub_in[...]
+        edge = pltpu.make_async_copy(sub_v, sub, sem.at[1])
+        edge.start()
         copy.wait()
-    sub_v[...] = sub_v[...] + sub_iv[...]
-    last = pltpu.make_async_copy(sub_v, sub, sem_c.at[blocks])
-    last.start()
-    for k in range(blocks):
-        out(k).wait()
-    last.wait()
+        edge.wait()
+
+    pl.run_scoped(run, pltpu.SemaphoreType.DMA((2,)))
 
 
 def shards(pair_density, trial_vectors, frequency, val_energy, cond_energy, pair_index):
@@ -515,20 +483,21 @@
     wide = 2 * grid_here
     trial = trial_vectors.reshape(width, grid_here)
     dma = pltpu.SemaphoreType.DMA
+    vmem = pl.BlockSpec(memory_space=pltpu.VMEM)
     anywhere = pl.BlockSpec(memory_space=pl.ANY)
     statics = (groups, members, chunks, freqs, vecs, rows, grid_here, prefactor, 1.0 / grid_count)
     semaphores = (
-        dma((chunks + 4,)), dma((3,)), dma((chunks, chips)), dma((chunks, chips)), dma((2,)), dma((1,)), dma((chunks, groups, chips)), dma((chunks, groups, chips)), dma((chips,)), dma((chips,)), dma((groups,)), dma((groups,)), dma((chunks, 2, chips)), dma((chunks, 2, chips)), dma((chunks, 2, chips)), dma((chunks, 2, chips)), dma((chunks,)), dma((chunks,)), dma((chunks, 2)), dma((chunks, 2)), dma((1,)), dma((1,)),
+        dma((chunks + 4,)), dma((chunks, chips)), dma((chunks, chips)), dma((2,)), dma((1,)), dma((chunks, groups, chips)), dma((chunks, groups, chips)), dma((chips,)), dma((chips,)), dma((groups,)), dma((groups,)), dma((chunks, 2, chips)), dma((chunks, 2, chips)), dma((chunks, 2, chips)), dma((chunks, 2, chips)), dma((chunks,)), dma((chunks,)), dma((chunks, 2)), dma((chunks, 2)), dma((1,)), dma((1,)),
     )
     parts = pl.pallas_call(
         functools.partial(kernel, statics, semaphores),
         out_shape=(
-            jax.ShapeDtypeStruct((width, grid_here), F32),
-            jax.ShapeDtypeStruct((width, vecs), F32),
-            jax.ShapeDtypeStruct((width, vecs), F32),
+            pltpu.VMEM((width, grid_here), F32),
+            pltpu.VMEM((width, vecs), F32),
+            pltpu.VMEM((width, vecs), F32),
         ),
         in_specs=[anywhere] * 6,
-        out_specs=(anywhere,) * 3,
+        out_specs=(vmem,) * 3,
         scratch_shapes=[
             pltpu.SMEM(frequency.shape, F32),
             pltpu.SMEM(val_energy.shape, F32),
@@ -536,7 +505,6 @@
             pltpu.VMEM((1, rows), jnp.int32),
             pltpu.VMEM((rows, 2, grid_count), BF16),
             pltpu.VMEM((chunks, 2 * piece, grid_count), BF16),
-            pltpu.VMEM((width, grid_here), F32),
             pltpu.VMEM((chunks, groups, chips, 2 * piece, wide), BF16),
             pltpu.VMEM((width, wide), BF16),
             pltpu.VMEM((8, 128), F32),
@@ -547,30 +515,29 @@
             pltpu.VMEM((chunks, 2, chips, slot, width // 2), BF16),
             pltpu.VMEM((chunks, 2, chips, slot, width // 2), BF16),
             pltpu.VMEM((freqs, 2 * vecs, 2 * vecs), F32),
-            pltpu.VMEM((width, vecs), F32),
             pltpu.VMEM((chunks, groups, chips, 2 * piece, grid_here), BF16),
             pltpu.VMEM((chunks, 2, chips, slot, width // 2), BF16),
         ],
         compiler_params=pltpu.CompilerParams(
-            collective_id=0, has_side_effects=True, vmem_limit_bytes=56 * 1024 * 1024
+            collective_id=0, has_side_effects=True, vmem_limit_bytes=40 * 1024 * 1024
         ),
-    )(pair_density, trial, frequency, val_energy, cond_energy, pair_index[None, :])
-    blocks = 4
+    )(
+        *(
+            pltpu.with_memory_space_constraint(x, pltpu.HBM)
+            for x in (pair_density, trial, frequency, val_energy, cond_energy, pair_index[None, :])
+        )
+    )
     images, sub = pl.pallas_call(
         closing,
         out_shape=(
             jax.ShapeDtypeStruct((width, grid_here), F32),
             jax.ShapeDtypeStruct((width, vecs), F32),
         ),
-        in_specs=[anywhere] * 3,
+        in_specs=[vmem] * 3,
         out_specs=(anywhere,) * 2,
-        scratch_shapes=[
-            pltpu.VMEM((width, grid_here), F32),
-            pltpu.VMEM((width, vecs), F32),
-            pltpu.VMEM((width, vecs), F32),
-            dma((blocks,)), dma((2,)), dma((blocks + 1,)),
-        ],
-    )(*parts)
+        scratch_shapes=[pltpu.VMEM((width, vecs), F32)],
+        compiler_params=pltpu.CompilerParams(vmem_limit_bytes=16 * 1024 * 1024),
+    )(*(pltpu.with_memory_space_constraint(x, pltpu.VMEM) for x in parts))
     return (
         images.reshape(freqs, 2, vecs, grid_here),
         sub.reshape(freqs, 2, vecs, vecs),

time: 61.9 us -> 59.5 us (0.961); the launches traced: 60.8 us -> 59.3 us
  Pallas kernels: 60.2 us -> 58.7 us
    pallas_call x1, Pallas kernels: 2.57 us -> 1.4 us  [shards(): pl.pallas_call(closing, out_shape=(jax.ShapeDtypeStruct((width, grid_here...]
where the time goes in v3:
time: 59.5 us; the launch traced here: 59.3 us
  Pallas kernels  58.7 us (99%)
  between operations  0.64 us (1%)
    pallas_call x1, Pallas kernels, shards(): pl.pallas_call(functools.partial(kernel, statics, semaphores), out_shape=...  57.3 us
    pallas_call x1, Pallas kernels, shards(): pl.pallas_call(closing, out_shape=(jax.ShapeDtypeStruct((width, grid_here...  1.4 us

profile of v3, /device:TPU:3, one launch (start us, length us, event | category | flops | bytes accessed | tf_op | source)
XLA Modules:
  0.0 59.3 jit_solution(10763874209531489324)
XLA Ops:
  0.6 57.3 %shard_map.77 = (f32[512,1024]{1,0:T(8,128)S(1)}, f32[512,64]{1,0:T(8,128)S(1)}, f32[512,64]{1,0:T(8,128)S(1)}) custom-call(bf16[32,2,8192]{2,1,0:T(2,128)(2,1)} %refs_0_.1, bf16[512,1024]{1,0:T(8,128)(2,1)} %bitcast.4, f32[4]{0:T(128)} %refs_2_.1, f32[32]{0:T(128)} %refs_3_.1, f32[32]{0:T(128)} %refs_4_.1, s32[1,32]{1,0:T(1,128)} %bitcast.5), custom_call_target="tpu_custom_call" | custom-call | tf_op jit(solution)/shard_map/pallas_call | solution.py:492
  57.9 1.4 %shard_map.78 = (f32[512,1024]{1,0:T(8,128)}, f32[512,64]{1,0:T(8,128)}) custom-call(f32[512,1024]{1,0:T(8,128)S(1)} %get-tuple-element.7.total, f32[512,64]{1,0:T(8,128)S(1)} %get-tuple-element.8.sub_mine, f32[512,64]{1,0:T(8,128)S(1)} %get-tuple-element.9.sub_in), custom_call_target="tpu_custom_call" | custom-call | tf_op jit(solution)/shard_map/pallas_call | solution.py:530

commit v4 on v3

--- a/solution.py
+++ b/solution.py
@@ -234,7 +234,6 @@
 
     def cross(j):
         arrive(j)
-        go(lend(j))
         over_grid = (((1,), (1,)), ((), ()))
         out = lax.dot_general(
             held[j].reshape(2 * chunk_rows, wide), both[...], over_grid, preferred_element_type=F32
@@ -248,6 +247,7 @@
             if split(j) or h == 1:
                 for s in range(1, chips):
                     go(slot_copy(j, h, s, (zc + s) % chips))
+        go(lend(j))
 
     def split(j):
         return j == chunks - 1
@@ -343,6 +343,12 @@
     def image(j, h):
         add(j, h, here(j, h) + lent(j, h))
 
+    def own_term(j, h):
+        add(j, h, here(j, h))
+
+    def lent_term(j, h):
+        add(j, h, lent(j, h))
+
     def last_own(h):
         add(chunks - 1, h, here(chunks - 1, h))
 
@@ -374,15 +380,15 @@
     for c in range(chunks):
         own_send(c)
     energies()
-    vectors_send()
     relay(0, own)
     relay(1, own)
     spread(0, one)
-    exchange(1)
     relay(2, own)
     spread(0, two)
+    exchange(1)
     relay(3, own)
     spread(0, rest)
+    vectors_send()
     relay(0, one)
     spread(1, one)
     relay(0, two)
@@ -415,10 +421,10 @@
     cross(2)
     scale(1, 0)
     scale(1, 1)
+    relay(3, rest)
     share(0, 0)
     squares(0, 0)
     squares(0, 1)
-    relay(3, rest)
     cross(3)
     scale(2, 0)
     scale(2, 1)
@@ -434,15 +440,17 @@
     share(2, 0)
     squares(2, 0)
     squares(2, 1)
-    image(2, 0)
-    image(2, 1)
+    own_term(2, 0)
+    own_term(2, 1)
     share(3, 0)
-    last_own(0)
+    own_term(3, 0)
     squares(3, 0)
     share(3, 1)
     squares(3, 1)
     last_sub()
-    last_own(1)
+    own_term(3, 1)
+    lent_term(2, 0)
+    lent_term(2, 1)
     last_lent(0)
     last_lent(1)
     last_wait()
@@ -456,15 +464,21 @@
 
 def closing(total, sub_mine, sub_in, images, sub, sub_v):
     def run(sem):
-        copy = pltpu.make_async_copy(total, images, sem.at[0])
-        copy.start()
+        size = total.shape[0] // 4
+        copies = [
+            pltpu.make_async_copy(total.at[pl.ds(k * size, size)], images.at[pl.ds(k * size, size)], sem.at[2 + k])
+            for k in range(4)
+        ]
+        for copy in copies:
+            copy.start()
         sub_v[...] = sub_mine[...] + sub_in[...]
         edge = pltpu.make_async_copy(sub_v, sub, sem.at[1])
         edge.start()
-        copy.wait()
+        for copy in copies:
+            copy.wait()
         edge.wait()
 
-    pl.run_scoped(run, pltpu.SemaphoreType.DMA((2,)))
+    pl.run_scoped(run, pltpu.SemaphoreType.DMA((6,)))
 
 
 def shards(pair_density, trial_vectors, frequency, val_energy, cond_energy, pair_index):

time: 59.5 us -> 59.2 us (level)
  Pallas kernels: 58.7 us -> 57.9 us
    pallas_call x1, Pallas kernels: 57.3 us -> 56.5 us  [shards(): pl.pallas_call(functools.partial(kernel, statics, semaphores), out_shape=...]
where the time goes in v4:
time: 59.2 us; the launch traced here: 58.5 us
  Pallas kernels  57.9 us (98%)
  between operations  0.64 us (1%)
    pallas_call x1, Pallas kernels, shards(): pl.pallas_call(functools.partial(kernel, statics, semaphores), out_shape=...  56.5 us
    pallas_call x1, Pallas kernels, shards(): pl.pallas_call(closing, out_shape=(jax.ShapeDtypeStruct((width, grid_here...  1.4 us

profile of v4, /device:TPU:3, one launch (start us, length us, event | category | flops | bytes accessed | tf_op | source)
XLA Modules:
  0.0 58.5 jit_solution(17343546492823989080)
XLA Ops:
  0.6 56.5 %shard_map.77 = (f32[512,1024]{1,0:T(8,128)S(1)}, f32[512,64]{1,0:T(8,128)S(1)}, f32[512,64]{1,0:T(8,128)S(1)}) custom-call(bf16[32,2,8192]{2,1,0:T(2,128)(2,1)} %refs_0_.1, bf16[512,1024]{1,0:T(8,128)(2,1)} %bitcast.4, f32[4]{0:T(128)} %refs_2_.1, f32[32]{0:T(128)} %refs_3_.1, f32[32]{0:T(128)} %refs_4_.1, s32[1,32]{1,0:T(1,128)} %bitcast.5), custom_call_target="tpu_custom_call" | custom-call | tf_op jit(solution)/shard_map/pallas_call | solution.py:506
  57.1 1.4 %shard_map.78 = (f32[512,1024]{1,0:T(8,128)}, f32[512,64]{1,0:T(8,128)}) custom-call(f32[512,1024]{1,0:T(8,128)S(1)} %get-tuple-element.7.total, f32[512,64]{1,0:T(8,128)S(1)} %get-tuple-element.8.sub_mine, f32[512,64]{1,0:T(8,128)S(1)} %get-tuple-element.9.sub_in), custom_call_target="tpu_custom_call" | custom-call | tf_op jit(solution)/shard_map/pallas_call | solution.py:544

commit v5 on v4

--- a/solution.py
+++ b/solution.py
@@ -19,7 +19,7 @@
     total_own, sub_out, sub_in,
     frequency, val_energy, cond_energy, pair_index,
     raw, packed, held, both, delta_own, freq_row, deltas, cols, ring_out, ring_in, scaled, acc,
-    held_p, scaled_p,
+    held_p, scaled_p, inverse,
     sem_in, sem_as, sem_ar, sem_os, sem_or, sem_fs, sem_fr, sem_ds, sem_dr, sem_es, sem_er,
     sem_rs, sem_rr, sem_gs, sem_gr, sem_ls, sem_lr, sem_qs, sem_qr, sem_is, sem_ir,
 ):
@@ -325,10 +325,17 @@
             preferred_element_type=F32,
         )
 
+    def invert():
+        for h in range(2):
+            inverse[h] = 1.0 / weights(cols[chunks - 1, :, 0:1], h)
+
     def squares(j, h):
         flat = scaled[j, h].reshape(chunk_rows, hw)
-        column = cols[j, :, 0:1]
-        crossing = (flat.astype(F32) / weights(column, h)).astype(BF16)
+        if split(j):
+            crossing = (flat.astype(F32) * inverse[h]).astype(BF16)
+        else:
+            column = cols[j, :, 0:1]
+            crossing = (flat.astype(F32) / weights(column, h)).astype(BF16)
         for i in range(freqs // 2):
             lo, hi = i * 2 * vecs, (i + 1) * 2 * vecs
             q = h * (freqs // 2) + i
@@ -430,6 +437,7 @@
     scale(2, 1)
     image(0, 0)
     image(0, 1)
+    invert()
     share(1, 0)
     squares(1, 0)
     squares(1, 1)
@@ -531,6 +539,7 @@
             pltpu.VMEM((freqs, 2 * vecs, 2 * vecs), F32),
             pltpu.VMEM((chunks, groups, chips, 2 * piece, grid_here), BF16),
             pltpu.VMEM((chunks, 2, chips, slot, width // 2), BF16),
+            pltpu.VMEM((2, chips * slot, width // 2), F32),
         ],
         compiler_params=pltpu.CompilerParams(
             collective_id=0, has_side_effects=True, vmem_limit_bytes=40 * 1024 * 1024

time: 59.2 us -> 59.1 us (level)
  no operation moved by 1% of the time
where the time goes in v5:
time: 59.1 us; the launch traced here: 58.4 us
  Pallas kernels  57.8 us (98%)
  between operations  0.64 us (1%)
    pallas_call x1, Pallas kernels, shards(): pl.pallas_call(functools.partial(kernel, statics, semaphores), out_shape=...  56.4 us
    pallas_call x1, Pallas kernels, shards(): pl.pallas_call(closing, out_shape=(jax.ShapeDtypeStruct((width, grid_here...  1.4 us

profile of v5, /device:TPU:3, one launch (start us, length us, event | category | flops | bytes accessed | tf_op | source)
XLA Modules:
  0.0 58.4 jit_solution(4012530996102848474)
XLA Ops:
  0.6 56.4 %shard_map.77 = (f32[512,1024]{1,0:T(8,128)S(1)}, f32[512,64]{1,0:T(8,128)S(1)}, f32[512,64]{1,0:T(8,128)S(1)}) custom-call(bf16[32,2,8192]{2,1,0:T(2,128)(2,1)} %refs_0_.1, bf16[512,1024]{1,0:T(8,128)(2,1)} %bitcast.4, f32[4]{0:T(128)} %refs_2_.1, f32[32]{0:T(128)} %refs_3_.1, f32[32]{0:T(128)} %refs_4_.1, s32[1,32]{1,0:T(1,128)} %bitcast.5), custom_call_target="tpu_custom_call" | custom-call | tf_op jit(solution)/shard_map/pallas_call | solution.py:514
  57.0 1.4 %shard_map.78 = (f32[512,1024]{1,0:T(8,128)}, f32[512,64]{1,0:T(8,128)}) custom-call(f32[512,1024]{1,0:T(8,128)S(1)} %get-tuple-element.7.total, f32[512,64]{1,0:T(8,128)S(1)} %get-tuple-element.8.sub_mine, f32[512,64]{1,0:T(8,128)S(1)} %get-tuple-element.9.sub_in), custom_call_target="tpu_custom_call" | custom-call | tf_op jit(solution)/shard_map/pallas_call | solution.py:553
